TPU v7x, 32 devices: a whole 2x2x4 slice. The times are simulated.
32 devices in a mesh: gx: 4 (over y, x), gy: 4 (over z), gz: 2 (over core).
Axes of the slice: x: 2, y: 2, z: 4, core: 2. Of those that a mesh axis runs over, the one named last changes fastest.
Arguments:
- a_blocks: float32 [1664, 7, 128, 128], P(('gx', 'gy', 'gz')), as said below
- block_cols: int32 [1664, 7], P(('gx', 'gy', 'gz')), may hold values from 0 to 363, as said below
- agg_ids: int32 [1664], P(('gx', 'gy', 'gz')), may hold values from 0 to 51, as said below
- agg_counts: int32 [32], P(('gx', 'gy', 'gz')), may hold values from 1 to 52, as said below
- p0_blocks: float32 [1664, 6, 128], P(('gx', 'gy', 'gz')), may hold values from -6 to 6
- start_vec: float32 [1664, 128], P(('gx', 'gy', 'gz'))
Outputs:
- p_blocks: float32 [1664, 7, 6, 128], P(('gx', 'gy', 'gz'))
- p_cols: int32 [1664, 7], P(('gx', 'gy', 'gz'))
- power_vec: float32 [1664, 128], P(('gx', 'gy', 'gz'))
Inputs may be any that keep to these rules, and one draw needn't show every extreme that they name: `block_cols`: entry 0 of each block row names the row itself; every neighbour that an entry names exists. `agg_ids`: below the count of the row's own subdomain. `agg_counts`: some subdomain has 52 aggregates. `a_blocks`: block 0 of each block row has a positive diagonal.
All inputs are finite; a program needn't handle non-finite values.
Results may differ from a plain program's by a relative error of at most 0.0003.
Values sent between devices are 32-bit elements; how exact they have to be, the bound alone decides.
A program may use at most 128 MiB of HBM per device.

v0:
```python
import functools

import jax
import jax.numpy as jnp
from jax import lax
from jax.experimental import pallas as pl
from jax.experimental.pallas import tpu as pltpu
from jax.sharding import PartitionSpec as P

ITERS = 8
AXES = ("gx", "gy", "gz")
MESH = pl.DeviceIdType.MESH
NT = (((1,), (1,)), ((), ()))


def split_bf16(x):
    hi = x.astype(jnp.bfloat16)
    lo = (x - hi.astype(jnp.float32)).astype(jnp.bfloat16)
    return jnp.concatenate([hi, lo], axis=1)


def kernel(sizes, group, a_hbm, cols_s, cols_v, ids_v, count_s, p0_hbm, start_v,
           q_hbm, pcols_v, power_v, by_v,
           q_v, a_v, va, vb, p_t, diag, acc, meta, sums, meta_own, sums_own,
           a_sem, p0_sem, q_sem, v_send, v_recv, p_send, p_recv, m_send, m_recv, s_send, s_recv):
    nx, ny, nz = sizes
    n = nx * ny * nz
    rows, blocks, width, _ = a_v.shape
    ns = p0_hbm.shape[0]
    slot = p_t.shape[1] // 7
    ix, iy, iz = (lax.axis_index(a) for a in AXES)
    me = (ix * ny + iy) * nz + iz
    groups = rows // group
    f32 = jnp.float32

    def a_copy(g):
        return pltpu.make_async_copy(
            a_hbm.at[pl.ds(g * group, group)], a_v.at[pl.ds(g * group, group)], a_sem.at[g])

    p0_copy = pltpu.make_async_copy(p0_hbm, p_t.at[:, pl.ds(0, rows)], p0_sem)
    p0_copy.start()
    for g in range(groups):
        a_copy(g).start()

    others = []
    for dx in range(nx):
        for dy in range(ny):
            for dz in range(nz):
                if dx or dy or dz:
                    others.append({"gx": lax.rem(ix + dx, nx), "gy": lax.rem(iy + dy, ny),
                                   "gz": lax.rem(iz + dz, nz)})

    barrier = pltpu.get_barrier_semaphore()
    for where in others:
        pl.semaphore_signal(barrier, inc=1, device_id=where, device_id_type=MESH)

    for r in range(rows):
        va[r] = start_v[r:r + 1]
    meta_own[0:1] = jnp.full((1, width), count_s[0], jnp.int32)
    meta_own[0:1, 0:rows] = ids_v[...]
    meta[pl.ds(me, 1)] = meta_own[...][None]
    pl.semaphore_wait(barrier, n - 1)

    sides = []
    for axis, (name, count, at) in enumerate(zip(AXES, sizes, (ix, iy, iz))):
        if count > 1:
            sides.append((2 * axis + 1, 2 * axis + 2, at > 0, {name: at - 1}))
            sides.append((2 * axis + 2, 2 * axis + 1, at < count - 1, {name: at + 1}))

    def halo(table, send_sem, recv_sem):
        def copy(mine, theirs, where, at, size):
            return pltpu.make_async_remote_copy(
                src_ref=table.at[pl.ds(at, size)],
                dst_ref=table.at[pl.ds(theirs * rows + at, size)],
                send_sem=send_sem.at[mine], recv_sem=recv_sem.at[theirs],
                device_id=where, device_id_type=MESH)

        def start(at, size):
            for mine, theirs, exists, where in sides:
                @pl.when(exists)
                def _():
                    copy(mine, theirs, where, at, size).start()

        def wait():
            for mine, theirs, exists, where in sides:
                @pl.when(exists)
                def _():
                    copy(mine, theirs, where, 0, rows).wait_send()
                    copy(theirs, mine, where, 0, rows).wait_recv()

        return start, wait

    def p_copy(mine, theirs, where, at, size):
        return pltpu.make_async_remote_copy(
            src_ref=p_t.at[pl.ds(at, size), pl.ds(0, rows)],
            dst_ref=p_t.at[pl.ds(at, size), pl.ds(theirs * slot, rows)],
            send_sem=p_send.at[mine], recv_sem=p_recv.at[theirs],
            device_id=where, device_id_type=MESH)

    def p_start(at, size):
        for mine, theirs, exists, where in sides:
            @pl.when(exists)
            def _():
                p_copy(mine, theirs, where, at, size).start()

    def p_wait():
        for mine, theirs, exists, where in sides:
            @pl.when(exists)
            def _():
                p_copy(mine, theirs, where, 0, ns).wait_send()
                p_copy(theirs, mine, where, 0, ns).wait_recv()

    def spread(own, table, send_sem, recv_sem):
        for where in others:
            pltpu.make_async_remote_copy(
                src_ref=own, dst_ref=table.at[me], send_sem=send_sem, recv_sem=recv_sem,
                device_id=where, device_id_type=MESH).start()

    def spread_wait(table, send_sem, recv_sem):
        part = table.at[pl.ds(0, n - 1)]
        pltpu.make_async_copy(part, part, send_sem).wait()
        pltpu.make_async_copy(part, part, recv_sem).wait()

    tables = (va, vb)
    halos = [halo(tables[i], v_send.at[i], v_recv.at[i]) for i in range(2)]
    halos[0][0](0, rows)
    spread(meta_own, meta, m_send, m_recv)
    p0_copy.wait()
    early = max(1, 2 * ns // 3)
    p_start(0, early)
    halos[0][1]()

    ones = jnp.ones((16, 2 * width), jnp.bfloat16)

    def mix(src, g, first):
        for r in range(group):
            b = g * group + r
            total = a_v[b, 0] * src[b]
            for k in range(1, blocks):
                total = total + a_v[b, k] * src[cols_s[k, b]]
            acc[lax.rem(g, 2) * group + r] = split_bf16(total)
            if first:
                eye = (lax.broadcasted_iota(jnp.int32, (width, width), 0)
                       == lax.broadcasted_iota(jnp.int32, (width, width), 1))
                diag[b] = jnp.sum(jnp.where(eye, a_v[b, 0], 0.0), axis=0, keepdims=True)

    def finish(dst, g):
        for r in range(0, group, 2):
            take = min(2, group - r)
            rhs = jnp.concatenate([acc[lax.rem(g, 2) * group + r + i] for i in range(take)], axis=0)
            out = lax.dot_general(ones, rhs, NT, preferred_element_type=f32)
            for i in range(take):
                b = g * group + r + i
                dst[b] = out[0:1, i * width:(i + 1) * width] / diag[b]

    def operate(src, dst, first, send):
        if first:
            a_copy(0).wait()
        mix(src, 0, first)

        def body(g, c):
            if first:
                a_copy(g).wait()
            finish(dst, g - 1)
            mix(src, g, first)
            if send:
                send((g - 1) * group, group)
            return c

        lax.fori_loop(1, groups, body, 0)
        finish(dst, groups - 1)
        if send:
            send((groups - 1) * group, group)

    def product(b, c):
        for k in range(blocks):
            at = b
            if k:
                col = cols_s[k, b]
                at = col + (slot - rows) * (col // rows)
            p = p_t[:, at, :]
            p = jnp.concatenate([p, jnp.zeros((8 - ns % 8, width), f32)], axis=0)
            hi = p.astype(jnp.bfloat16).astype(f32)
            left = jnp.concatenate([hi, p - hi], axis=0).astype(jnp.bfloat16)
            left = jnp.concatenate([left, left], axis=1)
            out = lax.dot_general(left, split_bf16(a_v[b, k]), NT, preferred_element_type=f32)
            half = out.shape[0] // 2
            q_v[k, :, b, :] = (out[:half] + out[half:])[:ns]
        return c

    def columns():
        counts = meta[...][:, :, width - 1:]
        owner = lax.broadcasted_iota(jnp.int32, counts.shape, 0)
        slots = [(jnp.bool_(True), me)]
        for (name, count, at, stride) in zip(AXES, sizes, (ix, iy, iz), (ny * nz, nz, 1)):
            slots.append((at > 0, me - stride))
            slots.append((at < count - 1, me + stride))
        entries = []
        for exists, d in slots:
            d = jnp.where(exists, d, me)
            offset = jnp.sum(jnp.where(owner < d, counts, 0).astype(f32), axis=0)
            entries.append(meta[d].astype(f32) + offset)
        entries.append(jnp.zeros((1, width), f32))
        table = jnp.concatenate(entries, axis=0).T
        row = lax.broadcasted_iota(jnp.int32, (rows, rows), 0)
        for k in range(blocks):
            cols = cols_v[k:k + 1]
            found = jnp.zeros((rows, rows), f32)
            for s in range(len(slots)):
                found = found + jnp.where(cols - s * rows == row, table[:rows, s:s + 1], 0.0)
            pcols_v[k:k + 1] = (jnp.sum(found, axis=0, keepdims=True) * ns).astype(jnp.int32)

    def squares(table):
        own = table[0:rows]
        return jnp.sum(jnp.sum(own * own, axis=0), axis=1, keepdims=True)

    q_copy = pltpu.make_async_copy(q_v, q_hbm, q_sem)
    done = 0
    before = None
    for t in range(1, ITERS + 1):
        src, dst = tables[(t - 1) % 2], tables[t % 2]
        start, wait = halos[t % 2]
        operate(src, dst, t == 1, start if t < ITERS else None)
        if t == ITERS - 1:
            before = squares(dst)
        if t < ITERS:
            if t == 1:
                p_start(early, ns - early)
                spread_wait(meta, m_send, m_recv)
                columns()
            else:
                if t == 2:
                    p_wait()
                until = rows * (t - 1) // (ITERS - 2)
                lax.fori_loop(done, until, product, 0)
                done = until
            if t == ITERS - 1:
                q_copy.start()
            wait()

    last = tables[ITERS % 2]
    lane = lax.broadcasted_iota(jnp.int32, (1, width), 1)
    sums_own[...] = jnp.where(lane == 0, before, jnp.where(lane == 1, squares(last), 0.0))
    sums[pl.ds(me, 1)] = sums_own[...][None]
    spread(sums_own, sums, s_send, s_recv)
    spread_wait(sums, s_send, s_recv)
    totals = jnp.sum(sums[...], axis=0)
    total_before = jnp.sum(jnp.where(lane == 0, totals, 0.0), axis=1, keepdims=True)
    total_last = jnp.sum(jnp.where(lane == 1, totals, 0.0), axis=1, keepdims=True)
    last_norm = jnp.sqrt(total_last)
    spectral = last_norm / jnp.sqrt(total_before)
    damping = 4.0 / (3.0 * spectral)
    factor = jnp.sqrt(jnp.full((1, 1), n * rows * width, f32)) / last_norm
    for r in range(rows):
        power_v[r:r + 1] = last[r] * factor

    by_v[...] = -(damping / jnp.concatenate([diag[r] for r in range(rows)], axis=0))
    q_copy.wait()


def scale_kernel(q, p0, by, cols, power, p_out, cols_out, power_out):
    cols_out[...] = cols[...]
    power_out[...] = power[...]
    factor = by[...]
    for k in range(q.shape[0]):
        for c in range(q.shape[1]):
            scaled = factor * q[k, c]
            p_out[k, c] = scaled + p0[c] if k == 0 else scaled


def solution(mesh):
    sizes = tuple(mesh.shape[a] for a in AXES)
    n = sizes[0] * sizes[1] * sizes[2]

    def local(a_blocks, block_cols, agg_ids, agg_counts, p0_blocks, start_vec):
        rows, blocks, width, _ = a_blocks.shape
        ns = p0_blocks.shape[1]
        group = next(g for g in (13, 4, 2, 1) if rows % g == 0)
        vmem = pl.BlockSpec(memory_space=pltpu.VMEM)
        smem = pl.BlockSpec(memory_space=pltpu.SMEM)
        dma = pltpu.SemaphoreType.DMA
        f32 = jnp.float32
        assert rows < width
        p0_planes = p0_blocks.transpose(1, 0, 2)
        product, cols, power, by = pl.pallas_call(
            functools.partial(kernel, sizes, group),
            out_shape=(
                jax.ShapeDtypeStruct((blocks, ns, rows, width), f32),
                jax.ShapeDtypeStruct((blocks, rows), jnp.int32),
                jax.ShapeDtypeStruct((rows, width), f32),
                jax.ShapeDtypeStruct((rows, width), f32),
            ),
            in_specs=[pl.BlockSpec(memory_space=pl.ANY), smem, vmem, vmem, smem, pl.BlockSpec(memory_space=pl.ANY), vmem],
            out_specs=(pl.BlockSpec(memory_space=pl.ANY), vmem, vmem, vmem),
            scratch_shapes=[
                pltpu.VMEM((blocks, ns, rows, width), f32),
                pltpu.VMEM((rows, blocks, width, width), f32),
                pltpu.VMEM((7 * rows, 1, width), f32),
                pltpu.VMEM((7 * rows, 1, width), f32),
                pltpu.VMEM((ns, 7 * (-(-rows // 8) * 8), width), f32),
                pltpu.VMEM((rows, 1, width), f32),
                pltpu.VMEM((2 * group, width, 2 * width), jnp.bfloat16),
                pltpu.VMEM((n, 1, width), jnp.int32),
                pltpu.VMEM((n, 1, width), f32),
                pltpu.VMEM((1, width), jnp.int32),
                pltpu.VMEM((1, width), f32),
                dma((rows // group,)), dma, dma,
                dma((2, 7)), dma((2, 7)), dma((7,)), dma((7,)),
                dma, dma, dma, dma,
            ],
            compiler_params=pltpu.CompilerParams(
                collective_id=0, has_side_effects=True, vmem_limit_bytes=56 * 1024 * 1024),
        )(a_blocks, block_cols.T, block_cols.T, agg_ids[None], agg_counts,
          p0_planes, start_vec)
        product, cols, power = pl.pallas_call(
            scale_kernel,
            out_shape=(
                jax.ShapeDtypeStruct(product.shape, f32),
                jax.ShapeDtypeStruct(cols.shape, jnp.int32),
                jax.ShapeDtypeStruct(power.shape, f32),
            ),
            in_specs=[vmem] * 5,
            out_specs=(vmem, vmem, vmem),
        )(product, p0_planes, by, cols, power)
        return product.transpose(2, 0, 1, 3), cols.T, power

    part = P(AXES)
    return jax.shard_map(
        local, mesh=mesh, in_specs=(part,) * 6, out_specs=(part,) * 3, check_vma=False)
```

profile of v0, /device:TPU:0, one launch (start us, length us, event | category | flops | bytes accessed | tf_op | source)
XLA Modules:
  0.0 66.8 jit_solution(18378950714038339498)
XLA Ops:
  1.3 63.0 %shard_map.85 = (f32[7,6,52,128]{3,2,1,0:T(8,128)}, s32[7,52]{1,0:T(8,128)}, f32[52,128]{1,0:T(8,128)}, f32[52,128]{1,0:T(8,128)}) custom-call(f32[52,7,128,128]{3,2,1,0:T(8,128)} %a_hbm.1, s32[7,52]{1,0:T(8,128)} %bitcast.7, s32[7,52]{1,0:T(8,128)} %bitcast.8, s32[1,52]{1,0:T(1,128)} %bitcast.9, s32[1]{0:T(128)S(6)} %copy.9.count_s, f32[6,52,128]{2,1,0:T(8,128)} %bitcast.5, ...), custom_call_target="tpu_custom_call" | custom-call | tf_op jit(solution)/shard_map/pallas_call | solution.py:285
  64.3 2.5 %shard_map.86 = (f32[7,6,52,128]{3,2,1,0:T(8,128)}, s32[7,52]{1,0:T(8,128)}, f32[52,128]{1,0:T(8,128)}) custom-call(f32[7,6,52,128]{3,2,1,0:T(8,128)} %get-tuple-element.10.q, f32[6,52,128]{2,1,0:T(8,128)} %bitcast.6, f32[52,128]{1,0:T(8,128)} %get-tuple-element.11.by, s32[7,52]{1,0:T(8,128)} %get-tuple-element.12.cols, f32[52,128]{1,0:T(8,128)} %get-tuple-element.13.power), custom_call_target="tpu_custom_call" | custom-call | tf_op jit(solution)/shard_map/pallas_call | solution.py:315
where the time goes:
time: 67.1 us; the launch traced here: 66.8 us
  Pallas kernels  65.5 us (98%)
  between operations  1.29 us (2%)
    pallas_call x1, Pallas kernels, local(): pl.pallas_call(functools.partial(kernel, sizes, group), out_shape=(jax.Sh...  63 us
    pallas_call x1, Pallas kernels, local(): pl.pallas_call(scale_kernel, out_shape=(jax.ShapeDtypeStruct(product.shap...  2.51 us

commit v1 on v0

--- a/solution.py
+++ b/solution.py
@@ -19,9 +19,9 @@
     return jnp.concatenate([hi, lo], axis=1)
 
 
-def kernel(sizes, group, a_hbm, cols_s, cols_v, ids_v, count_s, p0_hbm, start_v,
+def kernel(sizes, plan, a_hbm, cols_s, cols_v, ids_v, count_s, p0_hbm, start_v,
            q_hbm, pcols_v, power_v, by_v,
-           q_v, a_v, va, vb, p_t, diag, acc, meta, sums, meta_own, sums_own,
+           q_v, a_v, va, vb, p_t, diag, w_t, s_v, hold, meta, sums, meta_own, sums_own,
            a_sem, p0_sem, q_sem, v_send, v_recv, p_send, p_recv, m_send, m_recv, s_send, s_recv):
     nx, ny, nz = sizes
     n = nx * ny * nz
@@ -30,16 +30,17 @@
     slot = p_t.shape[1] // 7
     ix, iy, iz = (lax.axis_index(a) for a in AXES)
     me = (ix * ny + iy) * nz + iz
-    groups = rows // group
+    load, group, vpu = plan
+    pairs = (group - vpu) // 2
     f32 = jnp.float32
 
     def a_copy(g):
         return pltpu.make_async_copy(
-            a_hbm.at[pl.ds(g * group, group)], a_v.at[pl.ds(g * group, group)], a_sem.at[g])
+            a_hbm.at[pl.ds(g * load, load)], a_v.at[pl.ds(g * load, load)], a_sem.at[g])
 
     p0_copy = pltpu.make_async_copy(p0_hbm, p_t.at[:, pl.ds(0, rows)], p0_sem)
     p0_copy.start()
-    for g in range(groups):
+    for g in range(rows // load):
         a_copy(g).start()
 
     others = []
@@ -67,28 +68,28 @@
             sides.append((2 * axis + 1, 2 * axis + 2, at > 0, {name: at - 1}))
             sides.append((2 * axis + 2, 2 * axis + 1, at < count - 1, {name: at + 1}))
 
-    def halo(table, send_sem, recv_sem):
-        def copy(mine, theirs, where, at, size):
-            return pltpu.make_async_remote_copy(
-                src_ref=table.at[pl.ds(at, size)],
-                dst_ref=table.at[pl.ds(theirs * rows + at, size)],
-                send_sem=send_sem.at[mine], recv_sem=recv_sem.at[theirs],
-                device_id=where, device_id_type=MESH)
-
-        def start(at, size):
-            for mine, theirs, exists, where in sides:
-                @pl.when(exists)
-                def _():
-                    copy(mine, theirs, where, at, size).start()
-
-        def wait():
-            for mine, theirs, exists, where in sides:
-                @pl.when(exists)
-                def _():
-                    copy(mine, theirs, where, 0, rows).wait_send()
-                    copy(theirs, mine, where, 0, rows).wait_recv()
-
-        return start, wait
+    tables = (va, vb)
+
+    def v_copy(turn, mine, theirs, where, at, size):
+        table = tables[turn]
+        return pltpu.make_async_remote_copy(
+            src_ref=table.at[pl.ds(at, size)],
+            dst_ref=table.at[pl.ds(theirs * rows + at, size)],
+            send_sem=v_send.at[turn, mine], recv_sem=v_recv.at[turn, theirs],
+            device_id=where, device_id_type=MESH)
+
+    def v_start(turn, at, size):
+        for mine, theirs, exists, where in sides:
+            @pl.when(exists)
+            def _():
+                v_copy(turn, mine, theirs, where, at, size).start()
+
+    def v_wait(turn):
+        for mine, theirs, exists, where in sides:
+            @pl.when(exists)
+            def _():
+                v_copy(turn, mine, theirs, where, 0, rows).wait_send()
+                v_copy(turn, theirs, mine, where, 0, rows).wait_recv()
 
     def p_copy(mine, theirs, where, at, size):
         return pltpu.make_async_remote_copy(
@@ -121,56 +122,96 @@
         pltpu.make_async_copy(part, part, send_sem).wait()
         pltpu.make_async_copy(part, part, recv_sem).wait()
 
-    tables = (va, vb)
-    halos = [halo(tables[i], v_send.at[i], v_recv.at[i]) for i in range(2)]
-    halos[0][0](0, rows)
+    v_start(0, 0, rows)
     spread(meta_own, meta, m_send, m_recv)
     p0_copy.wait()
     early = max(1, 2 * ns // 3)
     p_start(0, early)
-    halos[0][1]()
-
-    ones = jnp.ones((16, 2 * width), jnp.bfloat16)
-
-    def mix(src, g, first):
-        for r in range(group):
-            b = g * group + r
-            total = a_v[b, 0] * src[b]
-            for k in range(1, blocks):
-                total = total + a_v[b, k] * src[cols_s[k, b]]
-            acc[lax.rem(g, 2) * group + r] = split_bf16(total)
+    v_wait(0)
+
+    lanes = lax.broadcasted_iota(jnp.int32, (width, width), 1)
+    late = hold.shape[0]
+
+    def lane_sum(total):
+        return jnp.sum(total, axis=1, keepdims=True)
+
+    def mix(turn, b):
+        src = tables[1 - turn]
+        total = a_v[b, 0] * src[b]
+        for k in range(1, blocks):
+            total = total + a_v[b, k] * src[cols_s[k, b]]
+        return total
+
+    def pair(turn, g, p):
+        src = tables[1 - turn]
+        b = g * group + vpu + 2 * p
+        x = jnp.concatenate(
+            [jnp.concatenate([src[b + i] if k == 0 else src[cols_s[k, b + i]]
+                              for k in range(blocks)], axis=1) for i in range(2)], axis=0)
+        hi = x.astype(jnp.bfloat16).astype(f32)
+        left = jnp.concatenate([hi, x - hi, jnp.zeros((4, x.shape[1]), f32)], axis=0).astype(jnp.bfloat16)
+        left = jnp.concatenate([left, left], axis=1)
+        out = jnp.dot(left, w_t[g * pairs + p], preferred_element_type=f32)
+        out = out[0:2] + out[2:4]
+        for i in range(2):
+            r = vpu + 2 * p + i
+            tables[turn][b + i] = out[i:i + 1, i * width:(i + 1) * width] / diag[b + i]
+
+    def mix_block(turn, g, size, count, first):
+        if not first:
+            for p in range(pairs):
+                pair(turn, g, p)
+        packed = jnp.zeros((width, width), f32)
+        for r in range(count):
+            b = g * size + r
+            total = mix(turn, b)
+            if r < count - late:
+                packed = jnp.where(lanes == r, lane_sum(total), packed)
+            else:
+                hold[r - (count - late)] = total
             if first:
-                eye = (lax.broadcasted_iota(jnp.int32, (width, width), 0)
-                       == lax.broadcasted_iota(jnp.int32, (width, width), 1))
+                eye = lanes == lax.broadcasted_iota(jnp.int32, (width, width), 0)
                 diag[b] = jnp.sum(jnp.where(eye, a_v[b, 0], 0.0), axis=0, keepdims=True)
-
-    def finish(dst, g):
-        for r in range(0, group, 2):
-            take = min(2, group - r)
-            rhs = jnp.concatenate([acc[lax.rem(g, 2) * group + r + i] for i in range(take)], axis=0)
-            out = lax.dot_general(ones, rhs, NT, preferred_element_type=f32)
-            for i in range(take):
-                b = g * group + r + i
-                dst[b] = out[0:1, i * width:(i + 1) * width] / diag[b]
-
-    def operate(src, dst, first, send):
+        s_v[...] = packed
+
+    def finish_block(turn, g, size, count):
+        packed = s_v[...]
+        for i in range(late):
+            packed = jnp.where(lanes == count - late + i, lane_sum(hold[i]), packed)
+        out = packed.T
+        for r in range(count):
+            b = g * size + r
+            tables[turn][b] = out[r:r + 1] / diag[b]
+
+    def operate(turn, first, send):
+        size, count = (load, load) if first else (group, vpu)
         if first:
             a_copy(0).wait()
-        mix(src, 0, first)
+        mix_block(turn, 0, size, count, first)
 
         def body(g, c):
             if first:
                 a_copy(g).wait()
-            finish(dst, g - 1)
-            mix(src, g, first)
+            finish_block(turn, g - 1, size, count)
+            mix_block(turn, g, size, count, first)
             if send:
-                send((g - 1) * group, group)
+                v_start(turn, (g - 1) * size, size)
             return c
 
-        lax.fori_loop(1, groups, body, 0)
-        finish(dst, groups - 1)
+        lax.fori_loop(1, rows // size, body, 0)
+        finish_block(turn, rows // size - 1, size, count)
         if send:
-            send((groups - 1) * group, group)
+            v_start(turn, rows - size, size)
+
+    def turn_over(i, c):
+        b = i // pairs * group + vpu + 2 * lax.rem(i, pairs)
+        for k in range(blocks):
+            x = jnp.concatenate([a_v[b, k].T, a_v[b + 1, k].T], axis=1)
+            hi = x.astype(jnp.bfloat16)
+            lo = (x - hi.astype(f32)).astype(jnp.bfloat16)
+            w_t[i, k * width:(k + 1) * width] = hi
+            w_t[i, (blocks + k) * width:(blocks + k + 1) * width] = lo
+        return c
 
     def product(b, c):
         for k in range(blocks):
@@ -210,37 +251,44 @@
                 found = found + jnp.where(cols - s * rows == row, table[:rows, s:s + 1], 0.0)
             pcols_v[k:k + 1] = (jnp.sum(found, axis=0, keepdims=True) * ns).astype(jnp.int32)
 
-    def squares(table):
-        own = table[0:rows]
+    def squares(turn):
+        own = tables[turn][0:rows]
         return jnp.sum(jnp.sum(own * own, axis=0), axis=1, keepdims=True)
 
     q_copy = pltpu.make_async_copy(q_v, q_hbm, q_sem)
-    done = 0
-    before = None
-    for t in range(1, ITERS + 1):
-        src, dst = tables[(t - 1) % 2], tables[t % 2]
-        start, wait = halos[t % 2]
-        operate(src, dst, t == 1, start if t < ITERS else None)
-        if t == ITERS - 1:
-            before = squares(dst)
-        if t < ITERS:
-            if t == 1:
-                p_start(early, ns - early)
-                spread_wait(meta, m_send, m_recv)
-                columns()
-            else:
-                if t == 2:
-                    p_wait()
-                until = rows * (t - 1) // (ITERS - 2)
-                lax.fori_loop(done, until, product, 0)
-                done = until
-            if t == ITERS - 1:
-                q_copy.start()
-            wait()
-
-    last = tables[ITERS % 2]
+    operate(1, True, True)
+    p_start(early, ns - early)
+    lax.fori_loop(0, w_t.shape[0], turn_over, 0)
+    spread_wait(meta, m_send, m_recv)
+    columns()
+    v_wait(1)
+
+    def step(t, turn):
+        operate(turn, False, True)
+
+        @pl.when(t == 2)
+        def _():
+            p_wait()
+
+        lax.fori_loop(rows * (t - 2) // (ITERS - 2), rows * (t - 1) // (ITERS - 2), product, 0)
+
+        @pl.when(t == ITERS - 1)
+        def _():
+            q_copy.start()
+
+        v_wait(turn)
+
+    def steps(i, c):
+        for turn in range(2):
+            step(2 * i + turn, turn)
+        return c
+
+    lax.fori_loop(1, ITERS // 2, steps, 0)
+    before = squares((ITERS - 1) % 2)
+    operate(ITERS % 2, False, False)
+
     lane = lax.broadcasted_iota(jnp.int32, (1, width), 1)
-    sums_own[...] = jnp.where(lane == 0, before, jnp.where(lane == 1, squares(last), 0.0))
+    sums_own[...] = jnp.where(lane == 0, before, jnp.where(lane == 1, squares(ITERS % 2), 0.0))
     sums[pl.ds(me, 1)] = sums_own[...][None]
     spread(sums_own, sums, s_send, s_recv)
     spread_wait(sums, s_send, s_recv)
@@ -252,7 +300,7 @@
     damping = 4.0 / (3.0 * spectral)
     factor = jnp.sqrt(jnp.full((1, 1), n * rows * width, f32)) / last_norm
     for r in range(rows):
-        power_v[r:r + 1] = last[r] * factor
+        power_v[r:r + 1] = tables[ITERS % 2][r] * factor
 
     by_v[...] = -(damping / jnp.concatenate([diag[r] for r in range(rows)], axis=0))
     q_copy.wait()
@@ -275,7 +323,10 @@
     def local(a_blocks, block_cols, agg_ids, agg_counts, p0_blocks, start_vec):
         rows, blocks, width, _ = a_blocks.shape
         ns = p0_blocks.shape[1]
-        group = next(g for g in (13, 4, 2, 1) if rows % g == 0)
+        load = next(g for g in (13, 4, 2, 1) if rows % g == 0)
+        group = 2 * load if rows % (2 * load) == 0 else load
+        vpu = group - group * 4 // 13 // 2 * 2
+        late = min(3, load, vpu)
         vmem = pl.BlockSpec(memory_space=pltpu.VMEM)
         smem = pl.BlockSpec(memory_space=pltpu.SMEM)
         dma = pltpu.SemaphoreType.DMA
@@ -283,7 +334,7 @@
         assert rows < width
         p0_planes = p0_blocks.transpose(1, 0, 2)
         product, cols, power, by = pl.pallas_call(
-            functools.partial(kernel, sizes, group),
+            functools.partial(kernel, sizes, (load, group, vpu)),
             out_shape=(
                 jax.ShapeDtypeStruct((blocks, ns, rows, width), f32),
                 jax.ShapeDtypeStruct((blocks, rows), jnp.int32),
@@ -299,12 +350,14 @@
                 pltpu.VMEM((7 * rows, 1, width), f32),
                 pltpu.VMEM((ns, 7 * (-(-rows // 8) * 8), width), f32),
                 pltpu.VMEM((rows, 1, width), f32),
-                pltpu.VMEM((2 * group, width, 2 * width), jnp.bfloat16),
+                pltpu.VMEM((rows // group * ((group - vpu) // 2), 2 * blocks * width, 2 * width), jnp.bfloat16),
+                pltpu.VMEM((width, width), f32),
+                pltpu.VMEM((late, width, width), f32),
                 pltpu.VMEM((n, 1, width), jnp.int32),
                 pltpu.VMEM((n, 1, width), f32),
                 pltpu.VMEM((1, width), jnp.int32),
                 pltpu.VMEM((1, width), f32),
-                dma((rows // group,)), dma, dma,
+                dma((rows // load,)), dma, dma,
                 dma((2, 7)), dma((2, 7)), dma((7,)), dma((7,)),
                 dma, dma, dma, dma,
             ],

time: 67.1 us -> 64.1 us (0.955)
  Pallas kernels: 65.5 us -> 62.6 us
    pallas_call x1, Pallas kernels: 63 us -> 60.1 us  [local(): pl.pallas_call(functools.partial(kernel, sizes, (load, group, vpu)), out_...]
where the time goes in v1:
time: 64.1 us; the launch traced here: 63.9 us
  Pallas kernels  62.6 us (98%)
  between operations  1.29 us (2%)
    pallas_call x1, Pallas kernels, local(): pl.pallas_call(functools.partial(kernel, sizes, (load, group, vpu)), out_...  60.1 us
    pallas_call x1, Pallas kernels, local(): pl.pallas_call(scale_kernel, out_shape=(jax.ShapeDtypeStruct(product.shap...  2.51 us

profile of v1, /device:TPU:0, one launch (start us, length us, event | category | flops | bytes accessed | tf_op | source)
XLA Modules:
  0.0 63.9 jit_solution(8008414432561433896)
XLA Ops:
  1.3 60.1 %shard_map.85 = (f32[7,6,52,128]{3,2,1,0:T(8,128)}, s32[7,52]{1,0:T(8,128)}, f32[52,128]{1,0:T(8,128)}, f32[52,128]{1,0:T(8,128)}) custom-call(f32[52,7,128,128]{3,2,1,0:T(8,128)} %a_hbm.1, s32[7,52]{1,0:T(8,128)} %bitcast.7, s32[7,52]{1,0:T(8,128)} %bitcast.8, s32[1,52]{1,0:T(1,128)} %bitcast.9, s32[1]{0:T(128)S(6)} %copy.9.count_s, f32[6,52,128]{2,1,0:T(8,128)} %bitcast.5, ...), custom_call_target="tpu_custom_call" | custom-call | tf_op jit(solution)/shard_map/pallas_call | solution.py:336
  61.4 2.5 %shard_map.86 = (f32[7,6,52,128]{3,2,1,0:T(8,128)}, s32[7,52]{1,0:T(8,128)}, f32[52,128]{1,0:T(8,128)}) custom-call(f32[7,6,52,128]{3,2,1,0:T(8,128)} %get-tuple-element.10.q, f32[6,52,128]{2,1,0:T(8,128)} %bitcast.6, f32[52,128]{1,0:T(8,128)} %get-tuple-element.11.by, s32[7,52]{1,0:T(8,128)} %get-tuple-element.12.cols, f32[52,128]{1,0:T(8,128)} %get-tuple-element.13.power), custom_call_target="tpu_custom_call" | custom-call | tf_op jit(solution)/shard_map/pallas_call | solution.py:368

commit v2 on v1

--- a/solution.py
+++ b/solution.py
@@ -8,6 +8,7 @@
 from jax.sharding import PartitionSpec as P
 
 ITERS = 8
+SPREAD = ITERS - 3
 AXES = ("gx", "gy", "gz")
 MESH = pl.DeviceIdType.MESH
 NT = (((1,), (1,)), ((), ()))
@@ -19,10 +20,10 @@
     return jnp.concatenate([hi, lo], axis=1)
 
 
-def kernel(sizes, plan, a_hbm, cols_s, cols_v, ids_v, count_s, p0_hbm, start_v,
-           q_hbm, pcols_v, power_v, by_v,
-           q_v, a_v, va, vb, p_t, diag, w_t, s_v, hold, meta, sums, meta_own, sums_own,
-           a_sem, p0_sem, q_sem, v_send, v_recv, p_send, p_recv, m_send, m_recv, s_send, s_recv):
+def kernel(sizes, plan, a_hbm, cols_hbm, ids_hbm, count_hbm, p0_hbm, start_hbm,
+           q_v, own_v, pcols_v, power_v, by_v,
+           cols_s, cols_v, ids_v, count_s, start_v, a_v, va, vb, p_t, diag, w_t, s_v, hold, meta, sums, meta_own, sums_own,
+           a_sem, p0_sem, in_sem, v_send, v_recv, p_send, p_recv, m_send, m_recv, s_send, s_recv):
     nx, ny, nz = sizes
     n = nx * ny * nz
     rows, blocks, width, _ = a_v.shape
@@ -39,6 +40,10 @@
             a_hbm.at[pl.ds(g * load, load)], a_v.at[pl.ds(g * load, load)], a_sem.at[g])
 
     p0_copy = pltpu.make_async_copy(p0_hbm, p_t.at[:, pl.ds(0, rows)], p0_sem)
+    inputs = [pltpu.make_async_copy(a, b, in_sem.at[i]) for i, (a, b) in enumerate((
+        (start_hbm, start_v), (ids_hbm, ids_v), (count_hbm, count_s), (cols_hbm, cols_s), (cols_hbm, cols_v)))]
+    for copy in inputs:
+        copy.start()
     p0_copy.start()
     for g in range(rows // load):
         a_copy(g).start()
@@ -48,25 +53,38 @@
         for dy in range(ny):
             for dz in range(nz):
                 if dx or dy or dz:
-                    others.append({"gx": lax.rem(ix + dx, nx), "gy": lax.rem(iy + dy, ny),
-                                   "gz": lax.rem(iz + dz, nz)})
-
+                    others.append(((dx > 0) + (dy > 0), {
+                        "gx": lax.rem(ix + dx, nx), "gy": lax.rem(iy + dy, ny), "gz": lax.rem(iz + dz, nz)}))
+    others = [where for _, where in sorted(others, key=lambda o: -o[0])]
+
+    sides = []
+    for axis, (name, count, at) in enumerate(zip(AXES, sizes, (ix, iy, iz))):
+        if count > 1:
+            sides.append((2 * axis + 1, 2 * axis + 2, at > 0, {name: at - 1}))
+            sides.append((2 * axis + 2, 2 * axis + 1, at < count - 1, {name: at + 1}))
+
+    near = nx + ny + nz - 3 <= SPREAD + 2
     barrier = pltpu.get_barrier_semaphore()
-    for where in others:
-        pl.semaphore_signal(barrier, inc=1, device_id=where, device_id_type=MESH)
-
+    if near:
+        for _, _, exists, where in sides:
+            @pl.when(exists)
+            def _():
+                pl.semaphore_signal(barrier, inc=1, device_id=where, device_id_type=MESH)
+    else:
+        for where in others:
+            pl.semaphore_signal(barrier, inc=1, device_id=where, device_id_type=MESH)
+
+    for copy in inputs:
+        copy.wait()
     for r in range(rows):
         va[r] = start_v[r:r + 1]
     meta_own[0:1] = jnp.full((1, width), count_s[0], jnp.int32)
     meta_own[0:1, 0:rows] = ids_v[...]
     meta[pl.ds(me, 1)] = meta_own[...][None]
-    pl.semaphore_wait(barrier, n - 1)
-
-    sides = []
-    for axis, (name, count, at) in enumerate(zip(AXES, sizes, (ix, iy, iz))):
-        if count > 1:
-            sides.append((2 * axis + 1, 2 * axis + 2, at > 0, {name: at - 1}))
-            sides.append((2 * axis + 2, 2 * axis + 1, at < count - 1, {name: at + 1}))
+    if near:
+        pl.semaphore_wait(barrier, sum(exists.astype(jnp.int32) for _, _, exists, _ in sides))
+    else:
+        pl.semaphore_wait(barrier, n - 1)
 
     tables = (va, vb)
 
@@ -123,11 +141,10 @@
         pltpu.make_async_copy(part, part, recv_sem).wait()
 
     v_start(0, 0, rows)
-    spread(meta_own, meta, m_send, m_recv)
     p0_copy.wait()
-    early = max(1, 2 * ns // 3)
-    p_start(0, early)
+    first, second = ns // 3, 2 * ns // 3
     v_wait(0)
+    p_start(0, first)
 
     lanes = lax.broadcasted_iota(jnp.int32, (width, width), 1)
     late = hold.shape[0]
@@ -213,8 +230,10 @@
             w_t[i, (blocks + k) * width:(blocks + k + 1) * width] = lo
         return c
 
-    def product(b, c):
-        for k in range(blocks):
+    each = 2 - rows % 2
+
+    def product(i, c):
+        for b, k in [(i * each + r, k) for r in range(each) for k in range(blocks)]:
             at = b
             if k:
                 col = cols_s[k, b]
@@ -255,28 +274,37 @@
         own = tables[turn][0:rows]
         return jnp.sum(jnp.sum(own * own, axis=0), axis=1, keepdims=True)
 
-    q_copy = pltpu.make_async_copy(q_v, q_hbm, q_sem)
     operate(1, True, True)
-    p_start(early, ns - early)
     lax.fori_loop(0, w_t.shape[0], turn_over, 0)
-    spread_wait(meta, m_send, m_recv)
-    columns()
+    p_start(first, second - first)
     v_wait(1)
 
     def step(t, turn):
         operate(turn, False, True)
 
+        @pl.when(t == 3)
+        def _():
+            p_wait()
+            own_v[...] = p_t[:, 0:rows]
+
+        @pl.when(t >= 3)
+        def _():
+            lax.fori_loop(rows // each * (t - 3) // (ITERS - 3), rows // each * (t - 2) // (ITERS - 3), product, 0)
+
+        @pl.when(t == ITERS - 1)
+        def _():
+            spread_wait(meta, m_send, m_recv)
+            columns()
+
+        v_wait(turn)
+
         @pl.when(t == 2)
         def _():
-            p_wait()
-
-        lax.fori_loop(rows * (t - 2) // (ITERS - 2), rows * (t - 1) // (ITERS - 2), product, 0)
-
-        @pl.when(t == ITERS - 1)
+            p_start(second, ns - second)
+
+        @pl.when(t == SPREAD)
         def _():
-            q_copy.start()
-
-        v_wait(turn)
+            spread(meta_own, meta, m_send, m_recv)
 
     def steps(i, c):
         for turn in range(2):
@@ -303,17 +331,21 @@
         power_v[r:r + 1] = tables[ITERS % 2][r] * factor
 
     by_v[...] = -(damping / jnp.concatenate([diag[r] for r in range(rows)], axis=0))
-    q_copy.wait()
-
-
-def scale_kernel(q, p0, by, cols, power, p_out, cols_out, power_out):
-    cols_out[...] = cols[...]
-    power_out[...] = power[...]
+
+
+def scale_kernel(q, p0, by, cols, power, p_hbm, cols_hbm, power_hbm, p_v, p_sem, sem):
+    small = [pltpu.make_async_copy(a, b, sem.at[i]) for i, (a, b) in enumerate(((cols, cols_hbm), (power, power_hbm)))]
+    for copy in small:
+        copy.start()
     factor = by[...]
-    for k in range(q.shape[0]):
+    copies = [pltpu.make_async_copy(p_v.at[k], p_hbm.at[k], p_sem.at[k]) for k in range(q.shape[0])]
+    for k, copy in enumerate(copies):
         for c in range(q.shape[1]):
             scaled = factor * q[k, c]
-            p_out[k, c] = scaled + p0[c] if k == 0 else scaled
+            p_v[k, c] = scaled + p0[c] if k == 0 else scaled
+        copy.start()
+    for copy in small + copies:
+        copy.wait()
 
 
 def solution(mesh):
@@ -328,23 +360,28 @@
         vpu = group - group * 4 // 13 // 2 * 2
         late = min(3, load, vpu)
         vmem = pl.BlockSpec(memory_space=pltpu.VMEM)
-        smem = pl.BlockSpec(memory_space=pltpu.SMEM)
         dma = pltpu.SemaphoreType.DMA
         f32 = jnp.float32
         assert rows < width
         p0_planes = p0_blocks.transpose(1, 0, 2)
-        product, cols, power, by = pl.pallas_call(
+        hbm = pl.BlockSpec(memory_space=pl.ANY)
+        product, own, cols, power, by = pl.pallas_call(
             functools.partial(kernel, sizes, (load, group, vpu)),
             out_shape=(
-                jax.ShapeDtypeStruct((blocks, ns, rows, width), f32),
-                jax.ShapeDtypeStruct((blocks, rows), jnp.int32),
-                jax.ShapeDtypeStruct((rows, width), f32),
-                jax.ShapeDtypeStruct((rows, width), f32),
+                pltpu.VMEM((blocks, ns, rows, width), f32),
+                pltpu.VMEM((ns, rows, width), f32),
+                pltpu.VMEM((blocks, rows), jnp.int32),
+                pltpu.VMEM((rows, width), f32),
+                pltpu.VMEM((rows, width), f32),
             ),
-            in_specs=[pl.BlockSpec(memory_space=pl.ANY), smem, vmem, vmem, smem, pl.BlockSpec(memory_space=pl.ANY), vmem],
-            out_specs=(pl.BlockSpec(memory_space=pl.ANY), vmem, vmem, vmem),
+            in_specs=[pl.BlockSpec(memory_space=pltpu.HBM)] * 6,
+            out_specs=(vmem,) * 5,
             scratch_shapes=[
-                pltpu.VMEM((blocks, ns, rows, width), f32),
+                pltpu.SMEM((blocks, rows), jnp.int32),
+                pltpu.VMEM((blocks, rows), jnp.int32),
+                pltpu.VMEM((1, rows), jnp.int32),
+                pltpu.SMEM((1,), jnp.int32),
+                pltpu.VMEM((rows, width), f32),
                 pltpu.VMEM((rows, blocks, width, width), f32),
                 pltpu.VMEM((7 * rows, 1, width), f32),
                 pltpu.VMEM((7 * rows, 1, width), f32),
@@ -357,14 +394,13 @@
                 pltpu.VMEM((n, 1, width), f32),
                 pltpu.VMEM((1, width), jnp.int32),
                 pltpu.VMEM((1, width), f32),
-                dma((rows // load,)), dma, dma,
+                dma((rows // load,)), dma, dma((5,)),
                 dma((2, 7)), dma((2, 7)), dma((7,)), dma((7,)),
                 dma, dma, dma, dma,
             ],
             compiler_params=pltpu.CompilerParams(
-                collective_id=0, has_side_effects=True, vmem_limit_bytes=56 * 1024 * 1024),
-        )(a_blocks, block_cols.T, block_cols.T, agg_ids[None], agg_counts,
-          p0_planes, start_vec)
+                collective_id=0, has_side_effects=True, vmem_limit_bytes=(67043328 - 1470 * 1024)),
+        )(a_blocks, block_cols.T, agg_ids[None], agg_counts, p0_planes, start_vec)
         product, cols, power = pl.pallas_call(
             scale_kernel,
             out_shape=(
@@ -373,8 +409,10 @@
                 jax.ShapeDtypeStruct(power.shape, f32),
             ),
             in_specs=[vmem] * 5,
-            out_specs=(vmem, vmem, vmem),
-        )(product, p0_planes, by, cols, power)
+            out_specs=(hbm,) * 3,
+            scratch_shapes=[pltpu.VMEM(product.shape, f32), dma((blocks,)), dma((2,))],
+            compiler_params=pltpu.CompilerParams(vmem_limit_bytes=8 * 1024 * 1024),
+        )(product, own, by, cols, power)
         return product.transpose(2, 0, 1, 3), cols.T, power
 
     part = P(AXES)

time: 64.1 us -> 60.7 us (0.947)
  Pallas kernels: 62.6 us -> 59.3 us
    pallas_call x1, Pallas kernels: 60.1 us -> 58.2 us  [local(): pl.pallas_call(functools.partial(kernel, sizes, (load, group, vpu)), out_...]
    pallas_call x1, Pallas kernels: 2.51 us -> 1.09 us  [local(): pl.pallas_call(scale_kernel, out_shape=(jax.ShapeDtypeStruct(product.shap...]
where the time goes in v2:
time: 60.7 us; the launch traced here: 60.6 us
  Pallas kernels  59.3 us (98%)
  between operations  1.29 us (2%)
    pallas_call x1, Pallas kernels, local(): pl.pallas_call(functools.partial(kernel, sizes, (load, group, vpu)), out_...  58.2 us

profile of v2, /device:TPU:0, one launch (start us, length us, event | category | flops | bytes accessed | tf_op | source)
XLA Modules:
  0.0 60.6 jit_solution(11005177122687996889)
XLA Ops:
  1.3 58.2 %shard_map.85 = (f32[7,6,52,128]{3,2,1,0:T(8,128)S(1)}, f32[6,52,128]{2,1,0:T(8,128)S(1)}, s32[7,52]{1,0:T(8,128)S(1)}, f32[52,128]{1,0:T(8,128)S(1)}, f32[52,128]{1,0:T(8,128)S(1)}) custom-call(f32[52,7,128,128]{3,2,1,0:T(8,128)} %a_hbm.1, s32[7,52]{1,0:T(8,128)} %bitcast.6, s32[1,52]{1,0:T(1,128)} %bitcast.7, s32[1]{0:T(128)S(6)} %copy.9.count_hbm, ...), custom_call_target="tpu_custom_call" | custom-call | tf_op jit(solution)/shard_map/pallas_call | solution.py:368
  59.5 1.1 %shard_map.86 = (f32[7,6,52,128]{3,2,1,0:T(8,128)}, s32[7,52]{1,0:T(8,128)}, f32[52,128]{1,0:T(8,128)}) custom-call(f32[7,6,52,128]{3,2,1,0:T(8,128)S(1)} %get-tuple-element.11.q, f32[6,52,128]{2,1,0:T(8,128)S(1)} %get-tuple-element.12.p0, f32[52,128]{1,0:T(8,128)S(1)} %get-tuple-element.13.by, s32[7,52]{1,0:T(8,128)S(1)} %get-tuple-element.14.cols, ...), custom_call_target="tpu_custom_call" | custom-call | tf_op jit(solution)/shard_map/pallas_call | solution.py:404

commit v3 on v2

--- a/solution.py
+++ b/solution.py
@@ -46,7 +46,7 @@
         copy.start()
     p0_copy.start()
     for g in range(rows // load):
-        a_copy(g).start()
+        a_copy(g).start(priority=1)
 
     others = []
     for dx in range(nx):
@@ -211,14 +211,19 @@
                 a_copy(g).wait()
             finish_block(turn, g - 1, size, count)
             mix_block(turn, g, size, count, first)
-            if send:
+            if first:
                 v_start(turn, (g - 1) * size, size)
             return c
 
         lax.fori_loop(1, rows // size, body, 0)
         finish_block(turn, rows // size - 1, size, count)
-        if send:
+        if first:
             v_start(turn, rows - size, size)
+        else:
+            if send is not True:
+                pl.when(send)(lambda: v_start(turn, 0, rows))
+            else:
+                v_start(turn, 0, rows)
 
     def turn_over(i, c):
         b = i // pairs * group + vpu + 2 * lax.rem(i, pairs)
@@ -279,9 +284,7 @@
     p_start(first, second - first)
     v_wait(1)
 
-    def step(t, turn):
-        operate(turn, False, True)
-
+    def between(t, turn):
         @pl.when(t == 3)
         def _():
             p_wait()
@@ -307,14 +310,18 @@
             spread(meta_own, meta, m_send, m_recv)
 
     def steps(i, c):
-        for turn in range(2):
-            step(2 * i + turn, turn)
+        operate(0, False, i < ITERS // 2)
+
+        @pl.when(i < ITERS // 2)
+        def _():
+            between(2 * i, 0)
+            operate(1, False, True)
+            between(2 * i + 1, 1)
+
         return c
 
-    lax.fori_loop(1, ITERS // 2, steps, 0)
+    lax.fori_loop(1, ITERS // 2 + 1, steps, 0)
     before = squares((ITERS - 1) % 2)
-    operate(ITERS % 2, False, False)
-
     lane = lax.broadcasted_iota(jnp.int32, (1, width), 1)
     sums_own[...] = jnp.where(lane == 0, before, jnp.where(lane == 1, squares(ITERS % 2), 0.0))
     sums[pl.ds(me, 1)] = sums_own[...][None]
@@ -355,9 +362,9 @@
     def local(a_blocks, block_cols, agg_ids, agg_counts, p0_blocks, start_vec):
         rows, blocks, width, _ = a_blocks.shape
         ns = p0_blocks.shape[1]
-        load = next(g for g in (13, 4, 2, 1) if rows % g == 0)
-        group = 2 * load if rows % (2 * load) == 0 else load
-        vpu = group - group * 4 // 13 // 2 * 2
+        load = next(g for g in (26, 4, 2, 1) if rows % g == 0)
+        group = next(g for g in (26, 13, 4, 2, 1) if rows % g == 0)
+        vpu = group - group * 3 // 13 // 2 * 2
         late = min(3, load, vpu)
         vmem = pl.BlockSpec(memory_space=pltpu.VMEM)
         dma = pltpu.SemaphoreType.DMA

time: 60.7 us -> 57 us (0.939)
  Pallas kernels: 59.3 us -> 55.5 us
    pallas_call x1, Pallas kernels: 58.2 us -> 54.4 us  [local(): pl.pallas_call(functools.partial(kernel, sizes, (load, group, vpu)), out_...]
where the time goes in v3:
time: 57 us; the launch traced here: 56.8 us
  Pallas kernels  55.5 us (97%)
  between operations  1.29 us (2%)
    pallas_call x1, Pallas kernels, local(): pl.pallas_call(functools.partial(kernel, sizes, (load, group, vpu)), out_...  54.4 us

profile of v3, /device:TPU:0, one launch (start us, length us, event | category | flops | bytes accessed | tf_op | source)
XLA Modules:
  0.0 56.8 jit_solution(590423250754278483)
XLA Ops:
  1.3 54.4 %shard_map.85 = (f32[7,6,52,128]{3,2,1,0:T(8,128)S(1)}, f32[6,52,128]{2,1,0:T(8,128)S(1)}, s32[7,52]{1,0:T(8,128)S(1)}, f32[52,128]{1,0:T(8,128)S(1)}, f32[52,128]{1,0:T(8,128)S(1)}) custom-call(f32[52,7,128,128]{3,2,1,0:T(8,128)} %a_hbm.1, s32[7,52]{1,0:T(8,128)} %bitcast.6, s32[1,52]{1,0:T(1,128)} %bitcast.7, s32[1]{0:T(128)S(6)} %copy.9.count_hbm, ...), custom_call_target="tpu_custom_call" | custom-call | tf_op jit(solution)/shard_map/pallas_call | solution.py:375
  55.7 1.1 %shard_map.86 = (f32[7,6,52,128]{3,2,1,0:T(8,128)}, s32[7,52]{1,0:T(8,128)}, f32[52,128]{1,0:T(8,128)}) custom-call(f32[7,6,52,128]{3,2,1,0:T(8,128)S(1)} %get-tuple-element.11.q, f32[6,52,128]{2,1,0:T(8,128)S(1)} %get-tuple-element.12.p0, f32[52,128]{1,0:T(8,128)S(1)} %get-tuple-element.13.by, s32[7,52]{1,0:T(8,128)S(1)} %get-tuple-element.14.cols, ...), custom_call_target="tpu_custom_call" | custom-call | tf_op jit(solution)/shard_map/pallas_call | solution.py:411
